TPU v7x, 32 devices: a whole 2x2x4 slice. The times are simulated.
32 devices in a mesh: mem: 4 (over z), lat: 2 (over y), lon: 4 (over x, core).
Axes of the slice: x: 2, y: 2, z: 4, core: 2. Of those that a mesh axis runs over, the one named last changes fastest.
Arguments:
- perturbations: bfloat16 [16, 8, 128, 1024], P('mem', None, 'lat', 'lon'), may hold values from -6 to 6
- increment: float32 [8, 128, 1024], P(None, 'lat', 'lon'), may hold values from -6 to 6
- taper_norm: float32 [8, 128, 1024], P(None, 'lat', 'lon'), may hold values from 1.5 to 6
- kappa: float32 [8], replicated, may hold values from 0.3 to 8
Outputs:
- covariance_product: float32 [8, 128, 1024], P('mem', 'lat', 'lon')
All inputs are finite; a program needn't handle non-finite values.
Results may differ from a plain program's by a relative error of at most 0.0003.
Values may be sent and summed in bfloat16 or wider, within the bound.
A program may use at most 64 MiB of HBM per device.

v0:
```python
import functools

import jax
import jax.numpy as jnp
from jax import lax
from jax.experimental import pallas as pl
from jax.experimental.pallas import tpu as pltpu
from jax.sharding import PartitionSpec as P

PASSES = 4
SWEEPS = 2
DEPTH = 2 * PASSES * SWEEPS
SUB = 8
LANES = 128
MESH = pl.DeviceIdType.MESH


def roll(value, shift):
    shift = shift % LANES
    return value if shift == 0 else pltpu.roll(value, shift, value.ndim - 1)


def kernel(
    sizes, kappa, pert, inc, taper, out,
    g, pack, rlon, cpack, rcor, rlat_p, rlat_g, nat, xs, ys, zs, part, rpart,
    lon_send, lon_recv, latp_send, latp_recv, latg_send, latg_recv,
    cor_send, cor_recv, part_send, part_recv,
):
    n_mem, n_lat, n_lon = sizes
    members, levels, rows, cols = pert.shape
    per = levels // n_mem
    pitch = nat.shape[1] // SUB
    step = (cols + 2 * DEPTH - LANES) // 2
    span = rows + (DEPTH if n_lat == 2 else 2 * DEPTH if n_lat > 2 else 0)
    mem, lat, lon = lax.axis_index("mem"), lax.axis_index("lat"), lax.axis_index("lon")
    base = 1 + jnp.where(lat == 0, DEPTH, 0) if n_lat <= 2 else 1
    lane = lax.broadcasted_iota(jnp.int32, (SUB, LANES), 1)
    sub = lax.broadcasted_iota(jnp.int32, (SUB, LANES), 0)
    lon_to = [lax.rem(lon + 1, n_lon), lax.rem(lon + n_lon - 1, n_lon)]
    lat_to = [lat + 1, lat - 1]
    sends = [lat < n_lat - 1, lat > 0]
    gets = [lat > 0, lat < n_lat - 1]
    edge = [rows - DEPTH, 0]

    def group(t):
        return lax.rem(mem + 1 + t, n_mem)

    def remote(src, dst, send, recv, **where):
        return pltpu.make_async_remote_copy(
            src_ref=src, dst_ref=dst, send_sem=send, recv_sem=recv,
            device_id=where, device_id_type=MESH,
        )

    def lon_copy(t, b):
        return remote(pack.at[b, t], rlon.at[b, t], lon_send.at[b, t], lon_recv.at[b, t],
                      mem=mem, lat=lat, lon=lon_to[b])

    def cor_copy(t, a, b):
        return remote(cpack.at[a, b, t], rcor.at[a, b, t], cor_send.at[a, b, t],
                      cor_recv.at[a, b, t], mem=mem, lat=lat_to[a], lon=lon_to[b])

    def latp_copy(t, a):
        return remote(pert.at[:, pl.ds(group(t) * per, per), pl.ds(edge[a], DEPTH), :],
                      rlat_p.at[a, t], latp_send.at[a, t], latp_recv.at[a, t],
                      mem=mem, lat=lat_to[a], lon=lon)

    def latg_copy(t, a):
        return remote(g.at[pl.ds(group(t) * per, per), pl.ds(edge[a], DEPTH), :],
                      rlat_g.at[a, t], latg_send.at[a, t], latg_recv.at[a, t],
                      mem=mem, lat=lat_to[a], lon=lon)

    def part_copy(t):
        return remote(part.at[t], rpart.at[t], part_send.at[t], part_recv.at[t],
                      mem=group(t), lat=lat, lon=lon)

    barrier = pltpu.get_barrier_semaphore()

    def greet(**where):
        pl.semaphore_signal(barrier, inc=1, device_id=where, device_id_type=MESH)

    for b in range(2):
        greet(mem=mem, lat=lat, lon=lon_to[b])
    for t in range(n_mem - 1):
        greet(mem=group(t), lat=lat, lon=lon)
    for a in range(2):
        @pl.when(sends[a])
        def _():
            greet(mem=mem, lat=lat_to[a], lon=lon)
            for b in range(2):
                greet(mem=mem, lat=lat_to[a], lon=lon_to[b])

    g[...] = taper[...] * inc[...]
    for buf in (xs, ys, zs):
        buf[...] = jnp.zeros_like(buf)

    beside = sum(jnp.where(s, 1, 0) for s in sends)
    pl.semaphore_wait(barrier, 2 + (n_mem - 1) + 3 * beside)

    def send_group(t, carry):
        e = group(t)
        for a in range(2):
            @pl.when(sends[a])
            def _():
                latg_copy(t, a).start()
                latp_copy(t, a).start()
        for b, column in enumerate((cols - LANES, 0)):
            source = LANES - DEPTH if b == 0 else 0
            corners = [[None] * (SUB * 2 * DEPTH // LANES) for _ in range(2)]
            for s in range(SUB):
                m, l = s // per, s % per
                w = pert[m, e * per + l, :, pl.ds(column, LANES)].astype(jnp.float32)
                w = w * g[e * per + l, :, pl.ds(column, LANES)]
                acc = None
                for q in range(rows // SUB):
                    v = roll(w[q * SUB : (q + 1) * SUB], q * DEPTH - source)
                    acc = v if acc is None else jnp.where(lane >= q * DEPTH, v, acc)
                pack[b, t, s] = acc
                each = LANES // (2 * DEPTH)
                j, i = s // each, s % each
                for a in range(2):
                    start = (edge[a] // SUB) * DEPTH
                    v = roll(acc, i * 2 * DEPTH - start)
                    old = corners[a][j]
                    corners[a][j] = v if old is None else jnp.where(lane >= i * 2 * DEPTH, v, old)
            for a in range(2):
                for j, v in enumerate(corners[a]):
                    cpack[a, b, t, j] = v
            lon_copy(t, b).start()
            for a in range(2):
                @pl.when(sends[a])
                def _():
                    cor_copy(t, a, b).start()
        return carry

    lax.fori_loop(0, n_mem, send_group, 0)

    def place(s, row, x0, x1, low, high):
        at = pl.ds(s * pitch + row, SUB)
        nat[0, at, :] = jnp.where(lane < DEPTH, low, roll(x0, DEPTH))
        cut = LANES - (step - DEPTH)
        nat[1, at, :] = jnp.where(lane < cut, roll(x0, cut), roll(x1, cut))
        nat[2, at, :] = jnp.where(lane < LANES - DEPTH, roll(x1, -DEPTH), high)

    def windows(t):
        e = group(t)
        for s in range(SUB):
            m, l = s // per, s % per
            w = pert[m, e * per + l].astype(jnp.float32) * g[e * per + l]
            left, right = rlon[0, t, s], rlon[1, t, s]
            for q in range(rows // SUB):
                r = slice(q * SUB, (q + 1) * SUB)
                place(s, DEPTH + q * SUB, w[r, :LANES], w[r, LANES:],
                      roll(left, -q * DEPTH), roll(right, LANES - DEPTH - q * DEPTH))
        each = LANES // (2 * DEPTH)
        for a in range(2):
            first = 0 if a == 0 else DEPTH + rows

            @pl.when(gets[a])
            def _():
                for s in range(SUB):
                    m, l = s // per, s % per
                    j, i = s // each, s % each
                    w = rlat_p[a, t, m, l].astype(jnp.float32) * rlat_g[a, t, l]
                    left, right = rcor[a, 0, t, j], rcor[a, 1, t, j]
                    for h in range(DEPTH // SUB):
                        r = slice(h * SUB, (h + 1) * SUB)
                        at = i * 2 * DEPTH + h * DEPTH
                        place(s, first + h * SUB, w[r, :LANES], w[r, LANES:],
                              roll(left, -at), roll(right, LANES - DEPTH - at))

            @pl.when(jnp.logical_not(gets[a]))
            def _():
                zero = jnp.zeros((DEPTH, LANES), jnp.float32)
                for s in range(SUB):
                    for k in range(3):
                        nat[k, pl.ds(s * pitch + first, DEPTH), :] = zero

    def gather(i, carry):
        for k in range(3):
            for j in range(SUB):
                r = i * SUB + j
                xs[k, 1 + r] = nat[k, pl.ds(r, SUB, stride=pitch), :]
        return carry

    def scatter(i, carry):
        for k in range(3):
            for j in range(SUB):
                r = DEPTH + i * SUB + j
                nat[k, pl.ds(r, SUB, stride=pitch), :] = xs[k, 1 + r]
        return carry

    def sweep(field, source, coef, target):
        block = SUB
        for i in range(0, span, block):
            for k in range(3):
                x = field[k, pl.ds(base + i - 1, block + 2)]
                p = x[:-1] + roll(x[1:], 1)
                p = p[:-1] + roll(p[1:], -1)
                own = x[1:-1] if source is field else source[k, pl.ds(base + i, block)]
                target[k, pl.ds(base + i, block)] = p + coef * own
        if n_lat > 2:
            for a in range(2):
                @pl.when(jnp.logical_not(gets[a]))
                def _():
                    for k in range(3):
                        target[k, pl.ds(1 if a == 0 else 1 + DEPTH + rows, DEPTH)] = jnp.zeros(
                            (DEPTH, SUB, LANES), jnp.float32)

    def work(t, carry):
        e = group(t)
        for b in range(2):
            lon_copy(t, b).wait_recv()
        for a in range(2):
            @pl.when(gets[a])
            def _():
                latg_copy(t, a).wait_recv()
                latp_copy(t, a).wait_recv()
                for b in range(2):
                    cor_copy(t, a, b).wait_recv()
        windows(t)
        lax.fori_loop(0, (rows + 2 * DEPTH) // SUB, gather, 0)
        weight = jnp.zeros((SUB, LANES), jnp.float32)
        for s in range(SUB):
            weight = jnp.where(sub == s, kappa[e * per + s % per], weight)
        first = 1.0 / weight
        second = first * (4.0 + first)

        def two(i, c):
            sweep(xs, xs, first, ys)
            sweep(ys, xs, second, zs)
            sweep(zs, zs, first, ys)
            sweep(ys, zs, second, xs)
            return c

        lax.fori_loop(0, PASSES, two, 0)
        lax.fori_loop(0, rows // SUB, scatter, 0)
        cut = LANES - (step - DEPTH)
        for l in range(per):
            k1 = jnp.full((SUB, LANES), kappa[e * per + l], jnp.float32)
            factor = k1 / (1.0 + 4.0 * k1)
            power = jnp.ones_like(factor)
            for _ in range(2 * PASSES * SWEEPS):
                power = power * factor
            factor = power / (members * n_mem - 1)
            for q in range(0, rows, 2 * SUB):
                sums = [[0.0, 0.0], [0.0, 0.0]]
                for m in range(members):
                    s = m * per + l
                    v = pert[m, e * per + l, q : q + 2 * SUB, :].astype(jnp.float32)
                    for h in range(2):
                        at = pl.ds(s * pitch + DEPTH + q + h * SUB, SUB)
                        mid = roll(nat[1, at, :], cut)
                        low = jnp.where(lane < LANES - 2 * DEPTH, roll(nat[0, at, :], -DEPTH), mid)
                        high = jnp.where(lane < cut - DEPTH, mid, roll(nat[2, at, :], DEPTH))
                        r = slice(h * SUB, (h + 1) * SUB)
                        sums[h][0] = sums[h][0] + v[r, :LANES] * low
                        sums[h][1] = sums[h][1] + v[r, LANES:] * high
                for h in range(2):
                    at = pl.ds(q + h * SUB, SUB)
                    tap = taper[e * per + l, at, :]
                    part[t, l, at, :LANES] = sums[h][0] * tap[:, :LANES] * factor
                    part[t, l, at, LANES:] = sums[h][1] * tap[:, LANES:] * factor

        @pl.when(t < n_mem - 1)
        def _():
            part_copy(t).start()

        return carry

    lax.fori_loop(0, n_mem, work, 0)
    total = part[n_mem - 1]
    for t in range(n_mem - 1):
        part_copy(t).wait_recv()
        total = total + rpart[t]
    out[...] = total

    def drain(t, carry):
        for b in range(2):
            lon_copy(t, b).wait_send()
        for a in range(2):
            @pl.when(sends[a])
            def _():
                latg_copy(t, a).wait_send()
                latp_copy(t, a).wait_send()
                for b in range(2):
                    cor_copy(t, a, b).wait_send()
        return carry

    lax.fori_loop(0, n_mem, drain, 0)
    for t in range(n_mem - 1):
        part_copy(t).wait_send()


def local(sizes, perturbations, increment, taper_norm, kappa):
    n_mem, n_lat, n_lon = sizes
    members, levels, rows, cols = perturbations.shape
    per = levels // n_mem
    assert members * per == SUB and cols == 2 * LANES and rows * DEPTH == SUB * LANES
    f32 = jnp.float32
    full = rows + 2 * DEPTH
    pitch = full + SUB // 2
    tiles = SUB * 2 * DEPTH // LANES
    field = pltpu.VMEM((3, full + 2, SUB, LANES), f32)
    dma = pltpu.SemaphoreType.DMA
    vmem = pl.BlockSpec(memory_space=pltpu.VMEM)
    return pl.pallas_call(
        functools.partial(kernel, sizes),
        out_shape=jax.ShapeDtypeStruct((per, rows, cols), f32),
        in_specs=[pl.BlockSpec(memory_space=pltpu.SMEM), vmem, vmem, vmem],
        out_specs=vmem,
        scratch_shapes=[
            pltpu.VMEM((levels, rows, cols), f32),
            pltpu.VMEM((2, n_mem, SUB, SUB, LANES), f32),
            pltpu.VMEM((2, n_mem, SUB, SUB, LANES), f32),
            pltpu.VMEM((2, 2, n_mem, tiles, SUB, LANES), f32),
            pltpu.VMEM((2, 2, n_mem, tiles, SUB, LANES), f32),
            pltpu.VMEM((2, n_mem, members, per, DEPTH, cols), jnp.bfloat16),
            pltpu.VMEM((2, n_mem, per, DEPTH, cols), f32),
            pltpu.VMEM((3, SUB * pitch, LANES), f32),
            field, field, field,
            pltpu.VMEM((n_mem, per, rows, cols), f32),
            pltpu.VMEM((n_mem - 1, per, rows, cols), f32),
            dma((2, n_mem)), dma((2, n_mem)),
            dma((2, n_mem)), dma((2, n_mem)),
            dma((2, n_mem)), dma((2, n_mem)),
            dma((2, 2, n_mem)), dma((2, 2, n_mem)),
            dma((n_mem - 1,)), dma((n_mem - 1,)),
        ],
        compiler_params=pltpu.CompilerParams(collective_id=0, has_side_effects=True),
    )(kappa, perturbations, increment, taper_norm)


def solution(mesh):
    sizes = tuple(mesh.shape[name] for name in ("mem", "lat", "lon"))
    return jax.shard_map(
        functools.partial(local, sizes),
        mesh=mesh,
        in_specs=(P("mem", None, "lat", "lon"), P(None, "lat", "lon"), P(None, "lat", "lon"), P()),
        out_specs=P("mem", "lat", "lon"),
        check_vma=False,
    )
```

profile of v0, /device:TPU:0, one launch (start us, length us, event | category | flops | bytes accessed | tf_op | source)
XLA Modules:
  0.0 164.3 jit_solution(12926773987020950115)
XLA Ops:
  0.0 162.7 %shard_map.46 = f32[2,64,256]{2,1,0:T(8,128)} custom-call(f32[8]{0:T(128)} %kappa.1, bf16[4,8,64,256]{3,2,1,0:T(8,128)(2,1)} %pert.1, f32[8,64,256]{2,1,0:T(8,128)} %inc.1, f32[8,64,256]{2,1,0:T(8,128)} %taper.1), custom_call_target="tpu_custom_call" | custom-call | tf_op jit(solution)/shard_map/pallas_call | solution.py:306
  162.7 1.6 copy.6
where the time goes:
time: 164 us
  Pallas kernels  163 us (99%)
    pallas_call x1, Pallas kernels, local(): pl.pallas_call(functools.partial(kernel, sizes), out_shape=jax.ShapeDtype...  163 us

commit v1 on v0

--- a/solution.py
+++ b/solution.py
@@ -194,10 +194,10 @@
         for i in range(0, span, block):
             for k in range(3):
                 x = field[k, pl.ds(base + i - 1, block + 2)]
-                p = x[:-1] + roll(x[1:], 1)
-                p = p[:-1] + roll(p[1:], -1)
-                own = x[1:-1] if source is field else source[k, pl.ds(base + i, block)]
-                target[k, pl.ds(base + i, block)] = p + coef * own
+                mid = x[1:-1]
+                own = mid if source is field else source[k, pl.ds(base + i, block)]
+                beside = roll(mid, 1) + roll(mid, -1)
+                target[k, pl.ds(base + i, block)] = (x[2:] + x[:-2]) + coef * own + beside
         if n_lat > 2:
             for a in range(2):
                 @pl.when(jnp.logical_not(gets[a]))

time: 164 us -> 54.1 us (0.33)
  Pallas kernels: 163 us -> 52.3 us
    pallas_call x1, Pallas kernels: 163 us -> 52.3 us  [local(): pl.pallas_call(functools.partial(kernel, sizes), out_shape=jax.ShapeDtype...]
where the time goes in v1:
time: 54.1 us; the launch traced here: 53.9 us
  Pallas kernels  52.3 us (97%)
  local copies, waits for them, and re-layouts  1.57 us (3%)
    pallas_call x1, Pallas kernels, local(): pl.pallas_call(functools.partial(kernel, sizes), out_shape=jax.ShapeDtype...  52.3 us
    unnamed x1, local copies, waits for them, and re-layouts  1.57 us

profile of v1, /device:TPU:0, one launch (start us, length us, event | category | flops | bytes accessed | tf_op | source)
XLA Modules:
  0.0 53.9 jit_solution(6433796253398025213)
XLA Ops:
  0.0 52.3 %shard_map.46 = f32[2,64,256]{2,1,0:T(8,128)} custom-call(f32[8]{0:T(128)} %kappa.1, bf16[4,8,64,256]{3,2,1,0:T(8,128)(2,1)} %pert.1, f32[8,64,256]{2,1,0:T(8,128)} %inc.1, f32[8,64,256]{2,1,0:T(8,128)} %taper.1), custom_call_target="tpu_custom_call" | custom-call | tf_op jit(solution)/shard_map/pallas_call | solution.py:306
  52.3 1.6 %copy.6 = f32[2,64,256]{2,1,0:T(8,128)} copy(f32[2,64,256]{2,1,0:T(8,128)} %shard_map.46) | data formatting | bytes 262144
